TPU v7x, 32 devices: a whole 2x2x4 slice. The times are simulated.
32 devices in a mesh: comp: 2 (over x), gy: 4 (over z), gx: 4 (over y, core).
Axes of the slice: x: 2, y: 2, z: 4, core: 2. Of those that a mesh axis runs over, the one named last changes fastest.
Arguments:
- column_water: float32 [2, 16, 32, 512], P('comp', None, 'gy', 'gx'), may hold values from 0.2 to 2
- land_soil: float32 [2, 32, 512], P('comp', 'gy', 'gx'), may hold values from 0.1 to 0.9
- level_weight: float32 [16], replicated, may hold values from 0.01 to 0.1
- excess_weight: float32 [16], replicated, may hold values from 0.3 to 3
- soil_weight: float32 [16], replicated, may hold values from 0.3 to 3
- terrain_class: int32 [320, 5120], P('gy', 'gx'), may hold values from 0 to 15
- surface_head: float32 [2, 320, 5120], P('comp', 'gy', 'gx'), may hold values from 0 to 1
- conductivity: float32 [2, 320, 5120], P('comp', 'gy', 'gx'), may hold values from 0.02 to 0.22
- active_mask: int32 [2, 320, 5120], P('comp', 'gy', 'gx'), may hold values 0 or 1
- flow_code: int32 [2, 320, 5120], P('comp', 'gy', 'gx'), may hold values from 0 to 3
Outputs:
- coupled_state: float32 [2, 32, 512], P('comp', 'gy', 'gx')
All inputs are finite; a program needn't handle non-finite values. No bound on the sum of `active_mask` on one device may be relied on, other than what follows from the above.
Results may differ from a plain program's by a relative error of at most 0.0003.
Values sent between devices are 32-bit elements; how exact they have to be, the bound alone decides.
A program may use at most 64 MiB of HBM per device.

v0:
```python
import functools

import jax
import jax.numpy as jnp
from jax import lax
from jax.experimental import pallas as pl
from jax.experimental.pallas import tpu as pltpu
from jax.sharding import PartitionSpec as P

AGG = 10
NSUB = 8
SWEEPS = 2

diffusion_rate = 0.2
infiltration_rate = 0.05
drainage_rate = 0.1
half_point = 0.1
evaporation_scale = 0.5

LANE = 128
SUB = 8
MESH = pl.DeviceIdType.MESH
DIRS = ((-1, 0), (1, 0), (0, -1), (0, 1), (-1, -1), (-1, 1), (1, -1), (1, 1))
N, S, W, E, NW, NE, SW, SE = range(8)
OPP = (S, N, E, W, SE, SW, NE, NW)


def iota(shape, dim):
    return lax.broadcasted_iota(jnp.int32, shape, dim)


def pick(table, classes):
    values = [table[k] for k in range(table.shape[0])]
    bit = 1
    while len(values) > 1:
        odd = (classes & bit) != 0
        values = [
            jnp.where(odd, values[k + 1], values[k]) for k in range(0, len(values), 2)
        ]
        bit *= 2
    return values[0]


def halves(x):
    high = x.astype(jnp.bfloat16)
    return high, (x - high.astype(jnp.float32)).astype(jnp.bfloat16)


def kernel(
    ny, nx,
    lw, ewt, swt, water_in, soil_in, terrain_in, head_in, cond_in, active_in, code_in,
    out_ref,
    xi, xf, st, ps, wb, mb, pk, dg, mn, qb, qx, back_tx, back_rx, gather, spreadm,
    send, recv, local, hop,
):
    group = lax.axis_index("comp")
    gy = lax.axis_index("gy")
    gx = lax.axis_index("gx")
    rows, cols = terrain_in.shape
    lev = water_in.shape[1]
    crow, ccol = soil_in.shape[1], soil_in.shape[2]
    tiles = cols // LANE
    width = tiles + 1
    bands = rows // SUB + 2

    lane = iota((SUB, LANE), 1)
    sub = iota((SUB, LANE), 0)

    def exists(d):
        dy, dx = DIRS[d]
        return (gy + dy >= 0) & (gy + dy < ny) & (gx + dx >= 0) & (gx + dx < nx)

    def at(d):
        dy, dx = DIRS[d]
        return {"comp": group, "gy": gy + dy, "gx": gx + dx}

    partner = {"comp": 1 - group, "gy": gy, "gx": gx}

    def copy(src, dst, d, f):
        return pltpu.make_async_remote_copy(
            src_ref=src, dst_ref=dst, send_sem=send.at[d, f], recv_sem=recv.at[OPP[d], f],
            device_id=at(d), device_id_type=MESH,
        )

    def arrival(dst, d, f):
        return pltpu.make_async_remote_copy(
            src_ref=dst, dst_ref=dst, send_sem=send.at[d, f], recv_sem=recv.at[d, f],
            device_id=at(d), device_id_type=MESH,
        )

    fields = (
        (cond_in.at[0], xf.at[0]),
        (active_in.at[0], xi.at[1]),
        (code_in.at[0], xi.at[2]),
        (head_in.at[0], xf.at[1]),
        (terrain_in, xi.at[0]),
    )
    rfrom = {-1: (0, SUB), 0: (0, rows), 1: (rows - SUB, SUB)}
    cfrom = {-1: (0, LANE), 0: (0, cols), 1: (cols - LANE, LANE)}
    rslot = {-1: (0, SUB), 0: (SUB, rows), 1: (rows + SUB, SUB)}
    cslot = {-1: (cols + LANE, LANE), 0: (0, cols), 1: (cols, LANE)}

    def cut(ref, r, c):
        return ref.at[pl.ds(r[0], r[1]), pl.ds(c[0], c[1])]

    def part(ref, d):
        return cut(ref, rfrom[DIRS[d][0]], cfrom[DIRS[d][1]])

    def slot(ref, d):
        return cut(ref, rslot[DIRS[d][0]], cslot[DIRS[d][1]])

    own = ((SUB, rows), (0, cols))

    def local_copy(src, dst, k):
        return pltpu.make_async_copy(src, dst, local.at[k])

    terrain_load = local_copy(terrain_in, cut(xi.at[0], *own), 4)
    route_loads = [local_copy(f[0], cut(f[1], *own), k) for k, f in enumerate(fields[:4])]
    water_load = local_copy(water_in.at[0], wb.at[8], 0)
    soil_load = local_copy(soil_in.at[0], mb.at[8], 1)

    barrier = pltpu.get_barrier_semaphore()
    for d in range(8):
        @pl.when(exists(d))
        def _():
            pl.semaphore_signal(barrier, inc=1, device_id=at(d), device_id_type=MESH)
    pl.semaphore_signal(barrier, inc=1, device_id=partner, device_id_type=MESH)
    greeted = 1
    for d in range(8):
        greeted = greeted + exists(d).astype(jnp.int32)

    terrain_load.start()

    @pl.when(group == 0)
    def _():
        water_load.start()
        soil_load.start()

    @pl.when(group == 1)
    def _():
        for load in route_loads:
            load.start()

    pl.semaphore_wait(barrier, greeted)

    def land_first(d):
        out = [copy(soil_in.at[0], mb.at[OPP[d]], d, 1)]
        if d < 4:
            out.insert(0, copy(water_in.at[0], wb.at[OPP[d]], d, 0))
        return out

    def land_pack(d):
        return copy(pk.at[0 if DIRS[d][1] < 0 else 1], dg.at[OPP[d] - 4], d, 0)

    def land_mean(d):
        return copy(mn.at[8], mn.at[OPP[d]], d, 2)

    def route_sends(d):
        return [copy(part(f[0], d), slot(f[1], OPP[d]), d, k) for k, f in enumerate(fields)]

    q_send = pltpu.make_async_remote_copy(
        src_ref=qb.at[0], dst_ref=qb.at[1], send_sem=hop.at[0], recv_sem=hop.at[1],
        device_id=partner, device_id_type=MESH,
    )
    back_send = pltpu.make_async_remote_copy(
        src_ref=back_tx, dst_ref=back_rx, send_sem=hop.at[2], recv_sem=hop.at[3],
        device_id=partner, device_id_type=MESH,
    )

    def over(dirs, act):
        for d in dirs:
            @pl.when(exists(d))
            def _():
                act(d)

    def start_all(copies):
        for c in copies:
            c.start()

    @pl.when(group == 0)
    def _():
        over(range(8), lambda d: start_all(land_first(d)))

    @pl.when(group == 1)
    def _():
        over(range(8), lambda d: start_all(route_sends(d)))

    k10 = iota((LANE, ccol), 1) * AGG
    j0 = iota((LANE, ccol), 0)

    for c in range(tiles):
        j = j0 + c * LANE
        gather[c * LANE : (c + 1) * LANE, :] = jnp.where(
            (j >= k10) & (j < k10 + AGG), 1.0, 0.0
        ).astype(jnp.bfloat16)

    def means(first, second):
        parts = []
        for field in (first, second):
            high, low = [], []
            for tile in field:
                a, b = halves(tile)
                high.append(a)
                low.append(b)
            parts.append(jnp.concatenate(high, axis=1))
            parts.append(jnp.concatenate(low, axis=1))
        stacked = jnp.concatenate(parts, axis=0)
        y = jnp.dot(stacked, gather[...], preferred_element_type=jnp.float32)
        i10 = iota((crow, rows), 0) * AGG
        i = iota((crow, rows), 1)
        pool = jnp.where((i >= i10) & (i < i10 + AGG), 1.0, 0.0)
        total = []
        for k in (0, 2):
            z = y[k * rows : (k + 1) * rows] + y[(k + 1) * rows : (k + 2) * rows]
            total.append(
                jnp.dot(pool, z, preferred_element_type=jnp.float32, precision=lax.Precision.HIGHEST)
                * (1.0 / (AGG * AGG))
            )
        return total

    @pl.when(group == 0)
    def _():
        water_load.wait()
        packs = [jnp.zeros((SUB, LANE), jnp.float32), jnp.zeros((SUB, LANE), jnp.float32)]
        for l in range(lev):
            mine = (lane >= 8 * l) & (lane < 8 * l + 8)
            w = wb[8, l]
            packs[0] = jnp.where(mine, pltpu.roll(w, (8 * l) % LANE, 1), packs[0])
            packs[1] = jnp.where(mine, pltpu.roll(w, (8 * l + 8) % LANE, 1), packs[1])
        pk[0] = packs[0]
        pk[1] = packs[1]
        over(range(4, 8), lambda d: land_pack(d).start())

        terrain_load.wait()
        firsts, seconds = [], []
        for c in range(tiles):
            tc = xi[0, SUB : SUB + rows, c * LANE : (c + 1) * LANE]
            firsts.append(pick(ewt, tc))
            seconds.append(pick(swt, tc))
        mean_e, mean_s = means(firsts, seconds)
        mn[8, 0] = mean_e
        mn[8, 1] = mean_s
        over(range(8), lambda d: land_mean(d).start())

        soil_load.wait()
        over(range(4), lambda d: arrival(wb.at[d], d, 0).wait_recv())
        over(range(4, 8), lambda d: arrival(dg.at[d - 4], d, 0).wait_recv())
        over(range(8), lambda d: arrival(mb.at[d], d, 1).wait_recv())

        def valid(a, b):
            r = sub + (0 if a == 0 else jnp.where(sub < 4, crow, -crow))
            r = r + gy * crow
            k = lane + (0 if b == 0 else jnp.where(lane < 64, ccol, -ccol))
            k = k + gx * ccol
            return (r >= 0) & (r < ny * crow) & (k >= 0) & (k < nx * ccol)

        ok = [[valid(a, b) for b in range(2)] for a in range(2)]
        left = lane < 64
        upper = sub < 4

        def joined(get, corner, fill):
            t = [
                [get(8), jnp.where(left, get(E), get(W))],
                [jnp.where(upper, get(S), get(N)), corner],
            ]
            return [[jnp.where(ok[a][b], t[a][b], fill) for b in range(2)] for a in range(2)]

        def corners(get):
            return jnp.where(
                upper,
                jnp.where(left, get(SE), get(SW)),
                jnp.where(left, get(NE), get(NW)),
            )

        def smooth(t):
            new = [[None, None], [None, None]]
            down = [[pltpu.roll(t[a][b], 1, 0) for b in range(2)] for a in range(2)]
            up = [[pltpu.roll(t[a][b], SUB - 1, 0) for b in range(2)] for a in range(2)]
            right = [[pltpu.roll(t[a][b], 1, 1) for b in range(2)] for a in range(2)]
            lft = [[pltpu.roll(t[a][b], LANE - 1, 1) for b in range(2)] for a in range(2)]
            for a in range(2):
                for b in range(2):
                    around = (
                        jnp.where(sub == 0, down[1 - a][b], down[a][b])
                        + jnp.where(sub == SUB - 1, up[1 - a][b], up[a][b])
                        + jnp.where(lane == 0, right[a][1 - b], right[a][b])
                        + jnp.where(lane == LANE - 1, lft[a][1 - b], lft[a][b])
                    )
                    value = t[a][b] + diffusion_rate * (around - 4.0 * t[a][b])
                    new[a][b] = jnp.where(ok[a][b], value, 0.0)
            return new

        ce = jnp.where(upper, dg[SE - 4], dg[NE - 4])
        cw = jnp.where(upper, dg[SW - 4], dg[NW - 4])
        precip = [[0.0, 0.0], [0.0, 0.0]]
        ground = None
        for l in range(lev):
            corner = jnp.where(
                left,
                pltpu.roll(ce, (LANE - 8 * l) % LANE, 1),
                pltpu.roll(cw, (2 * LANE - 8 - 8 * l) % LANE, 1),
            )
            t = joined(lambda k: wb[k, l], corner, 0.0)
            for _ in range(SWEEPS):
                t = smooth(t)
            if l == 0:
                ground = t[0][0]
            for a in range(2):
                for b in range(2):
                    precip[a][b] = precip[a][b] + lw[l] * t[a][b] * t[a][b]

        moisture = joined(lambda k: mb[k], corners(lambda k: mb[k]), 0.5)
        over(range(8), lambda d: arrival(mn.at[d], d, 2).wait_recv())
        m_e = joined(lambda k: mn[k, 0], corners(lambda k: mn[k, 0]), 1.0)
        m_s = joined(lambda k: mn[k, 1], corners(lambda k: mn[k, 1]), 1.0)
        for a in range(2):
            for b in range(2):
                m = moisture[a][b]
                excess = precip[a][b] * m * m / (m * m + half_point)
                rs = slice(a * SUB, (a + 1) * SUB)
                cs = slice(b * LANE, (b + 1) * LANE)
                qb[0, 0, rs, cs] = excess / m_e[a][b]
                qb[0, 1, rs, cs] = m / m_s[a][b]
        q_send.start()
        divisor = 1.0 + evaporation_scale * ground * ground
        over(range(8), lambda d: [c.wait_send() for c in land_first(d)])
        over(range(4, 8), lambda d: land_pack(d).wait_send())
        over(range(8), lambda d: land_mean(d).wait_send())
        q_send.wait_send()
        back_send.wait_recv()
        out_ref[0] = back_rx[...] / divisor

    R, AD, M0, M1, M2, M3, EW, HD, SO = range(9)
    WN, WS, WW, WE, AA, B0, B1, B2, B3 = range(9, 18)

    @pl.when(group == 1)
    def _():
        kk = iota((2 * ccol, LANE), 0)
        jj = iota((2 * ccol, LANE), 1)
        for c in range(tiles):
            j = jj + c * LANE
            spreadm[:, c * LANE : (c + 1) * LANE] = jnp.where(
                (j >= kk * AGG) & (j < kk * AGG + AGG), 1.0, 0.0
            ).astype(jnp.bfloat16)
        spreadm[:, cols:] = jnp.where(
            ((jj < 64) & (kk == ccol)) | ((jj >= 64) & (kk == 2 * ccol - 1)), 1.0, 0.0
        ).astype(jnp.bfloat16)

        zero = jnp.zeros((SUB, LANE), jnp.float32)
        for c in range(width):
            for edge in (0, (bands + 1) * SUB):
                for k in (R, M0, M1):
                    st[k, c, edge : edge + SUB] = zero
                for k in range(2):
                    for p in range(2):
                        ps[p, k, c, edge : edge + SUB] = zero

        def prepare(t, c):
            r = pl.ds(t * SUB if isinstance(t, int) else pl.multiple_of(t * SUB, SUB), SUB)
            o = pl.ds(
                (t + 1) * SUB if isinstance(t, int) else pl.multiple_of(t * SUB + SUB, SUB), SUB
            )

            def take(ref, k):
                a = ref[k, r, c * LANE : (c + 1) * LANE]
                if c < tiles:
                    return a
                return jnp.where(lane < 64, a, ref[k, r, (c + 1) * LANE : (c + 2) * LANE])

            row = sub + (t - 1) * SUB + gy * rows
            col = lane + c * LANE
            if c == tiles:
                col = jnp.where(lane < 64, col, lane - LANE)
            col = col + gx * cols
            ok = (row >= 0) & (row < ny * rows) & (col >= 0) & (col < nx * cols)
            active = jnp.where(ok, take(xi, 1).astype(jnp.float32), 0.0)
            code = take(xi, 2)
            keff = jnp.where(ok, take(xf, 0), 0.0) * active
            tc = take(xi, 0)
            st[R, c, o] = jnp.sqrt(keff)
            rate = drainage_rate * active
            st[AD, c, o] = rate
            for k in range(4):
                st[M0 + k, c, o] = jnp.where(code == k, rate, 0.0)
            st[EW, c, o] = active * pick(ewt, tc)
            st[HD, c, o] = active * jnp.where(ok, take(xf, 1), 0.0)
            st[SO, c, o] = pick(swt, tc)

        for load in route_loads:
            load.wait()
        terrain_load.wait()

        def inner(t, carry):
            for c in range(tiles):
                prepare(t, c)
            return carry

        lax.fori_loop(1, bands - 1, inner, 0)

        over(range(8), lambda d: [arrival(slot(f[1], d), d, k).wait_recv() for k, f in enumerate(fields)])

        def rim(k, carry):
            for c in range(tiles):
                prepare(k * (bands - 1), c)
            return carry

        lax.fori_loop(0, 2, rim, 0)

        def side(t, carry):
            prepare(t, tiles)
            return carry

        lax.fori_loop(0, bands, side, 0)

        def from_west(tile_list):
            turned = [pltpu.roll(x, 1, 1) for x in tile_list]
            return [jnp.where(lane == 0, turned[c - 1], turned[c]) for c in range(width)]

        def from_east(tile_list):
            turned = [pltpu.roll(x, LANE - 1, 1) for x in tile_list]
            return [
                jnp.where(lane == LANE - 1, turned[(c + 1) % width], turned[c])
                for c in range(width)
            ]

        def couple(t, carry):
            base = pl.multiple_of(t * SUB + SUB, SUB)
            o = pl.ds(base, SUB)
            above = pl.ds(base - 1, SUB)
            below = pl.ds(base + 1, SUB)
            r = [st[R, c, o] for c in range(width)]
            west, east = from_west(r), from_east(r)
            for c in range(width):
                wn = r[c] * st[R, c, above]
                ws = r[c] * st[R, c, below]
                ww = r[c] * west[c]
                we = r[c] * east[c]
                st[WN, c, o] = wn
                st[WS, c, o] = ws
                st[WW, c, o] = ww
                st[WE, c, o] = we
                st[AA, c, o] = (wn + ws) + (ww + we)
                st[B0, c, o] = st[M0, c, below]
                st[B1, c, o] = st[M1, c, above]
            for c, v in enumerate(from_east([st[M2, c, o] for c in range(width)])):
                st[B2, c, o] = v
            for c, v in enumerate(from_west([st[M3, c, o] for c in range(width)])):
                st[B3, c, o] = v
            return carry

        lax.fori_loop(0, bands, couple, 0)

        q_send.wait_recv()
        high, low = [], []
        for k in range(2):
            a, b = halves(qb[1, k])
            high.append(a)
            low.append(b)
        y = jnp.dot(
            jnp.concatenate(high + low, axis=0), spreadm[...], preferred_element_type=jnp.float32
        )
        qx[...] = y[: 4 * SUB] + y[4 * SUB :]
        for t in range(bands):
            o = slice((t + 1) * SUB, (t + 2) * SUB)
            if t == 0:
                a = b = 2 * crow - 1
            elif t == bands - 1:
                a = b = crow
            else:
                a, b = ((t - 1) * SUB) // AGG, ((t - 1) * SUB + SUB - 1) // AGG
            for c in range(width):
                cs = slice(c * LANE, (c + 1) * LANE)

                def up(k):
                    first = jnp.broadcast_to(qx[k * 16 + a : k * 16 + a + 1, cs], (SUB, LANE))
                    if a == b:
                        return first
                    second = jnp.broadcast_to(qx[k * 16 + b : k * 16 + b + 1, cs], (SUB, LANE))
                    return jnp.where(sub < b * AGG - (t - 1) * SUB, first, second)

                ps[0, 0, c, o] = st[HD, c, o] + st[EW, c, o] * up(0)
                ps[0, 1, c, o] = st[SO, c, o] * up(1)

        def substep(src, dst):
            def band(t, carry):
                base = pl.multiple_of(t * SUB + SUB, SUB)
                o = pl.ds(base, SUB)
                above = pl.ds(base - 1, SUB)
                below = pl.ds(base + 1, SUB)
                p = [ps[src, 0, c, o] for c in range(width)]
                s = [ps[src, 1, c, o] for c in range(width)]
                ss = [x * x for x in s]
                p_w, p_e = from_west(p), from_east(p)
                s_w, s_e = from_west(ss), from_east(ss)
                for c in range(width):
                    s_n = ps[src, 1, c, above]
                    s_s = ps[src, 1, c, below]
                    spread = (
                        st[WN, c, o] * ps[src, 0, c, above]
                        + st[WS, c, o] * ps[src, 0, c, below]
                        + (st[WW, c, o] * p_w[c] + st[WE, c, o] * p_e[c])
                        - st[AA, c, o] * p[c]
                    )
                    soaked = infiltration_rate * p[c] * pl.reciprocal(1.0 + s[c])
                    inflow = (
                        st[B0, c, o] * (s_s * s_s)
                        + st[B1, c, o] * (s_n * s_n)
                        + (st[B2, c, o] * s_e[c] + st[B3, c, o] * s_w[c])
                        - st[AD, c, o] * ss[c]
                    )
                    ps[dst, 0, c, o] = p[c] + (spread - soaked)
                    ps[dst, 1, c, o] = s[c] + (soaked + inflow)
                return carry

            lax.fori_loop(0, bands, band, 0)

        def two(k, carry):
            substep(0, 1)
            substep(1, 0)
            return carry

        lax.fori_loop(0, NSUB // 2, two, 0)

        inside = slice(2 * SUB, 2 * SUB + rows)
        mean_p, mean_st = means(
            [ps[0, 0, c, inside] for c in range(tiles)],
            [ps[0, 1, c, inside] for c in range(tiles)],
        )
        back_tx[...] = mean_st
        back_send.start()
        out_ref[0] = mean_p
        over(range(8), lambda d: [c.wait_send() for c in route_sends(d)])
        back_send.wait_send()


def per_device(ny, nx, column_water, land_soil, level_weight, excess_weight, soil_weight,
               terrain_class, surface_head, conductivity, active_mask, flow_code):
    rows, cols = terrain_class.shape
    lev = column_water.shape[1]
    crow, ccol = land_soil.shape[1:]
    wide = cols // LANE + 1
    tall = rows + 4 * SUB
    f32, i32 = jnp.float32, jnp.int32
    any_spec = pl.BlockSpec(memory_space=pl.ANY)
    smem = pl.BlockSpec(memory_space=pltpu.SMEM)
    return pl.pallas_call(
        functools.partial(kernel, ny, nx),
        out_shape=jax.ShapeDtypeStruct((1, crow, ccol), f32),
        in_specs=[smem] * 3 + [any_spec] * 7,
        out_specs=pl.BlockSpec(memory_space=pltpu.VMEM),
        scratch_shapes=[
            pltpu.VMEM((3, rows + 2 * SUB, cols + 2 * LANE), i32),
            pltpu.VMEM((2, rows + 2 * SUB, cols + 2 * LANE), f32),
            pltpu.VMEM((18, wide, tall, LANE), f32),
            pltpu.VMEM((2, 2, wide, tall, LANE), f32),
            pltpu.VMEM((9, lev, crow, ccol), f32),
            pltpu.VMEM((9, crow, ccol), f32),
            pltpu.VMEM((2, crow, ccol), f32),
            pltpu.VMEM((4, crow, ccol), f32),
            pltpu.VMEM((9, 2, crow, ccol), f32),
            pltpu.VMEM((2, 2, 2 * crow, 2 * ccol), f32),
            pltpu.VMEM((4 * crow, cols + LANE), f32),
            pltpu.VMEM((crow, ccol), f32),
            pltpu.VMEM((crow, ccol), f32),
            pltpu.VMEM((cols, ccol), jnp.bfloat16),
            pltpu.VMEM((2 * ccol, cols + LANE), jnp.bfloat16),
            pltpu.SemaphoreType.DMA((8, 5)),
            pltpu.SemaphoreType.DMA((8, 5)),
            pltpu.SemaphoreType.DMA((5,)),
            pltpu.SemaphoreType.DMA((4,)),
        ],
        compiler_params=pltpu.CompilerParams(
            collective_id=0, has_side_effects=True, vmem_limit_bytes=48 * 1024 * 1024
        ),
    )(level_weight, excess_weight, soil_weight, column_water, land_soil, terrain_class,
      surface_head, conductivity, active_mask, flow_code)


def solution(mesh):
    in_specs = (
        P("comp", None, "gy", "gx"),
        P("comp", "gy", "gx"),
        P(),
        P(),
        P(),
        P("gy", "gx"),
        P("comp", "gy", "gx"),
        P("comp", "gy", "gx"),
        P("comp", "gy", "gx"),
        P("comp", "gy", "gx"),
    )
    body = functools.partial(per_device, mesh.shape["gy"], mesh.shape["gx"])
    return jax.shard_map(
        body, mesh=mesh, in_specs=in_specs, out_specs=P("comp", "gy", "gx"), check_vma=False
    )
```

profile of v0, /device:TPU:0, one launch (start us, length us, event | category | flops | bytes accessed | tf_op | source)
XLA Modules:
  0.0 39.7 jit_solution(6625006226380223577)
XLA Ops:
  0.0 0.0 copy-start
  0.0 1.0 %copy-done = s32[80,1280]{1,0:T(8,128)S(1)} copy-done((s32[80,1280]{1,0:T(8,128)S(1)}, s32[80,1280]{1,0:T(8,128)}, u32[]{:S(2)}) %copy-start) | copy-done | bytes 409624
  1.0 0.0 copy-start.1
  1.0 1.0 %copy-done.1 = f32[1,80,1280]{2,1,0:T(8,128)S(1)} copy-done((f32[1,80,1280]{2,1,0:T(8,128)S(1)}, f32[1,80,1280]{2,1,0:T(8,128)}, u32[]{:S(2)}) %copy-start.1) | copy-done | bytes 409624
  2.0 0.0 copy-start.2
  2.0 1.0 %copy-done.2 = f32[1,80,1280]{2,1,0:T(8,128)S(1)} copy-done((f32[1,80,1280]{2,1,0:T(8,128)S(1)}, f32[1,80,1280]{2,1,0:T(8,128)}, u32[]{:S(2)}) %copy-start.2) | copy-done | bytes 409624
  3.0 0.0 copy-start.3
  3.0 1.0 %copy-done.3 = s32[1,80,1280]{2,1,0:T(8,128)S(1)} copy-done((s32[1,80,1280]{2,1,0:T(8,128)S(1)}, s32[1,80,1280]{2,1,0:T(8,128)}, u32[]{:S(2)}) %copy-start.3) | copy-done | bytes 409624
  4.0 0.0 copy-start.4
  4.0 1.0 %copy-done.4 = s32[1,80,1280]{2,1,0:T(8,128)S(1)} copy-done((s32[1,80,1280]{2,1,0:T(8,128)S(1)}, s32[1,80,1280]{2,1,0:T(8,128)}, u32[]{:S(2)}) %copy-start.4) | copy-done | bytes 409624
  5.0 0.0 copy-start.5
  5.0 0.8 %copy-done.5 = f32[1,16,8,128]{3,2,1,0:T(8,128)S(1)} copy-done((f32[1,16,8,128]{3,2,1,0:T(8,128)S(1)}, f32[1,16,8,128]{3,2,1,0:T(8,128)}, u32[]{:S(2)}) %copy-start.5) | copy-done | bytes 65560
  5.9 0.0 copy-start.6
  5.9 0.7 %copy-done.6 = f32[1,8,128]{2,1,0:T(8,128)S(1)} copy-done((f32[1,8,128]{2,1,0:T(8,128)S(1)}, f32[1,8,128]{2,1,0:T(8,128)}, u32[]{:S(2)}) %copy-start.6) | copy-done | bytes 4120
  6.5 0.0 copy-start.7
  6.5 0.7 %copy-done.7 = f32[16]{0:T(128)S(1)} copy-done((f32[16]{0:T(128)S(1)}, f32[16]{0:T(128)}, u32[]{:S(2)}) %copy-start.7) | copy-done | bytes 88
  7.2 0.0 copy-start.8
  7.2 0.7 %copy-done.8 = f32[16]{0:T(128)S(1)} copy-done((f32[16]{0:T(128)S(1)}, f32[16]{0:T(128)}, u32[]{:S(2)}) %copy-start.8) | copy-done | bytes 88
  7.8 0.0 copy-start.9
  7.9 0.7 %copy-done.9 = f32[16]{0:T(128)S(1)} copy-done((f32[16]{0:T(128)S(1)}, f32[16]{0:T(128)}, u32[]{:S(2)}) %copy-start.9) | copy-done | bytes 88
  8.5 30.6 %shard_map.100 = f32[1,8,128]{2,1,0:T(8,128)S(1)} custom-call(f32[16]{0:T(128)S(1)} %copy-done.7, f32[16]{0:T(128)S(1)} %copy-done.8, f32[16]{0:T(128)S(1)} %copy-done.9, f32[1,16,8,128]{3,2,1,0:T(8,128)S(1)} %copy-done.5, f32[1,8,128]{2,1,0:T(8,128)S(1)} %copy-done.6, s32[80,1280]{1,0:T(8,128)S(1)} %copy-done, f32[1,80,1280]{2,1,0:T(8,128)S(1)} %copy-done.1, ...), custom_call_target="tpu_custom_call" | custom-call | tf_op jit(solution)/shard_map/pallas_call | solution.py:546
  39.2 0.6 %copy.12 = f32[1,8,128]{2,1,0:T(8,128)} copy(f32[1,8,128]{2,1,0:T(8,128)S(1)} %shard_map.100) | data formatting | bytes 8192
Async XLA Ops:
  0.0 1.0 %copy-start = (s32[80,1280]{1,0:T(8,128)S(1)}, s32[80,1280]{1,0:T(8,128)}, u32[]{:S(2)}) copy-start(s32[80,1280]{1,0:T(8,128)} %terrain_in.1) | copy-start | bytes 1228804
  1.0 1.0 %copy-start.1 = (f32[1,80,1280]{2,1,0:T(8,128)S(1)}, f32[1,80,1280]{2,1,0:T(8,128)}, u32[]{:S(2)}) copy-start(f32[1,80,1280]{2,1,0:T(8,128)} %head_in.1) | copy-start | bytes 1228804
  2.0 1.0 %copy-start.2 = (f32[1,80,1280]{2,1,0:T(8,128)S(1)}, f32[1,80,1280]{2,1,0:T(8,128)}, u32[]{:S(2)}) copy-start(f32[1,80,1280]{2,1,0:T(8,128)} %cond_in.1) | copy-start | bytes 1228804
  3.0 1.0 %copy-start.3 = (s32[1,80,1280]{2,1,0:T(8,128)S(1)}, s32[1,80,1280]{2,1,0:T(8,128)}, u32[]{:S(2)}) copy-start(s32[1,80,1280]{2,1,0:T(8,128)} %active_in.1) | copy-start | bytes 1228804
  4.0 1.0 %copy-start.4 = (s32[1,80,1280]{2,1,0:T(8,128)S(1)}, s32[1,80,1280]{2,1,0:T(8,128)}, u32[]{:S(2)}) copy-start(s32[1,80,1280]{2,1,0:T(8,128)} %code_in.1) | copy-start | bytes 1228804
  5.0 0.8 %copy-start.5 = (f32[1,16,8,128]{3,2,1,0:T(8,128)S(1)}, f32[1,16,8,128]{3,2,1,0:T(8,128)}, u32[]{:S(2)}) copy-start(f32[1,16,8,128]{3,2,1,0:T(8,128)} %water_in.1) | copy-start | bytes 196612
  5.9 0.7 %copy-start.6 = (f32[1,8,128]{2,1,0:T(8,128)S(1)}, f32[1,8,128]{2,1,0:T(8,128)}, u32[]{:S(2)}) copy-start(f32[1,8,128]{2,1,0:T(8,128)} %soil_in.1) | copy-start | bytes 12292
  6.5 0.7 %copy-start.7 = (f32[16]{0:T(128)S(1)}, f32[16]{0:T(128)}, u32[]{:S(2)}) copy-start(f32[16]{0:T(128)} %lw.1) | copy-start | bytes 196
  7.2 0.7 %copy-start.8 = (f32[16]{0:T(128)S(1)}, f32[16]{0:T(128)}, u32[]{:S(2)}) copy-start(f32[16]{0:T(128)} %ewt.1) | copy-start | bytes 196
  7.8 0.7 %copy-start.9 = (f32[16]{0:T(128)S(1)}, f32[16]{0:T(128)}, u32[]{:S(2)}) copy-start(f32[16]{0:T(128)} %swt.1) | copy-start | bytes 196
where the time goes:
time: 40.2 us; the launch traced here: 39.7 us
  Pallas kernels  30.6 us (76%)
  local copies, waits for them, and re-layouts  9.09 us (23%)
    pallas_call x1, Pallas kernels, per_device(): pl.pallas_call(functools.partial(kernel, ny, nx), out_shape=jax.ShapeDtyp...  30.6 us
    unnamed x21, local copies, waits for them, and re-layouts  9.09 us

commit v1 on v0

--- a/solution.py
+++ b/solution.py
@@ -395,7 +395,7 @@
                 prepare(t, c)
             return carry
 
-        lax.fori_loop(1, bands - 1, inner, 0)
+        lax.fori_loop(1, bands - 1, inner, 0, unroll=2)
 
         over(range(8), lambda d: [arrival(slot(f[1], d), d, k).wait_recv() for k, f in enumerate(fields)])
 
@@ -410,7 +410,7 @@
             prepare(t, tiles)
             return carry
 
-        lax.fori_loop(0, bands, side, 0)
+        lax.fori_loop(0, bands, side, 0, unroll=6)
 
         def from_west(tile_list):
             turned = [pltpu.roll(x, 1, 1) for x in tile_list]
@@ -448,7 +448,7 @@
                 st[B3, c, o] = v
             return carry
 
-        lax.fori_loop(0, bands, couple, 0)
+        lax.fori_loop(0, bands, couple, 0, unroll=4)
 
         q_send.wait_recv()
         high, low = [], []
@@ -512,7 +512,7 @@
                     ps[dst, 1, c, o] = s[c] + (soaked + inflow)
                 return carry
 
-            lax.fori_loop(0, bands, band, 0)
+            lax.fori_loop(0, bands, band, 0, unroll=12)
 
         def two(k, carry):
             substep(0, 1)
@@ -541,7 +541,7 @@
     wide = cols // LANE + 1
     tall = rows + 4 * SUB
     f32, i32 = jnp.float32, jnp.int32
-    any_spec = pl.BlockSpec(memory_space=pl.ANY)
+    any_spec = pl.BlockSpec(memory_space=pltpu.HBM)
     smem = pl.BlockSpec(memory_space=pltpu.SMEM)
     return pl.pallas_call(
         functools.partial(kernel, ny, nx),
@@ -570,7 +570,7 @@
             pltpu.SemaphoreType.DMA((4,)),
         ],
         compiler_params=pltpu.CompilerParams(
-            collective_id=0, has_side_effects=True, vmem_limit_bytes=48 * 1024 * 1024
+            collective_id=0, has_side_effects=True
         ),
     )(level_weight, excess_weight, soil_weight, column_water, land_soil, terrain_class,
       surface_head, conductivity, active_mask, flow_code)

time: 40.2 us -> 25.8 us (0.64)
  local copies, waits for them, and re-layouts: 9.09 us -> 1.28 us
  Pallas kernels: 30.6 us -> 24.3 us
    unnamed x21 -> x1, local copies, waits for them, and re-layouts: 9.09 us -> 1.28 us
    pallas_call x1, Pallas kernels: 30.6 us -> 24.3 us  [per_device(): pl.pallas_call(functools.partial(kernel, ny, nx), out_shape=jax.ShapeDtyp...]
where the time goes in v1:
time: 25.8 us; the launch traced here: 25.6 us
  Pallas kernels  24.3 us (94%)
  local copies, waits for them, and re-layouts  1.28 us (5%)
    pallas_call x1, Pallas kernels, per_device(): pl.pallas_call(functools.partial(kernel, ny, nx), out_shape=jax.ShapeDtyp...  24.3 us
    unnamed x1, local copies, waits for them, and re-layouts  1.28 us

profile of v1, /device:TPU:0, one launch (start us, length us, event | category | flops | bytes accessed | tf_op | source)
XLA Modules:
  0.0 25.6 jit_solution(2913359261365609760)
XLA Ops:
  0.0 24.3 %shard_map.100 = f32[1,8,128]{2,1,0:T(8,128)} custom-call(f32[16]{0:T(128)} %lw.1, f32[16]{0:T(128)} %ewt.1, f32[16]{0:T(128)} %swt.1, f32[1,16,8,128]{3,2,1,0:T(8,128)} %water_in.1, f32[1,8,128]{2,1,0:T(8,128)} %soil_in.1, s32[80,1280]{1,0:T(8,128)} %terrain_in.1, f32[1,80,1280]{2,1,0:T(8,128)} %head_in.1, f32[1,80,1280]{2,1,0:T(8,128)} %cond_in.1, ...), custom_call_target="tpu_custom_call" | custom-call | tf_op jit(solution)/shard_map/pallas_call | solution.py:546
  24.3 1.3 %copy.12 = f32[1,8,128]{2,1,0:T(8,128)} copy(f32[1,8,128]{2,1,0:T(8,128)} %shard_map.100) | data formatting | bytes 8192
